TPU v7x, 32 devices: a whole 2x2x4 slice. The times are simulated.
32 devices in a mesh: dp: 2 (over x), ep: 16 (over z, y, core).
Axes of the slice: x: 2, y: 2, z: 4, core: 2. Of those that a mesh axis runs over, the one named last changes fastest.
Arguments:
- tokens: bfloat16 [8192, 2048], P(('dp', 'ep')), parts along dimension 0
- expert_ids: int32 [8192, 6], P(('dp', 'ep')), parts along dimension 0
- gate_vals: float32 [8192, 6], P(('dp', 'ep')), parts along dimension 0
- w_gate: bfloat16 [64, 2048, 1408], P('ep')
- w_up: bfloat16 [64, 2048, 1408], P('ep')
- w_down: bfloat16 [64, 1408, 2048], P('ep')
Outputs:
- output: bfloat16 [8192, 2048], P(('dp', 'ep')), parts along dimension 0
There are 2 independent parts. A program takes and returns all parts, laid end to end along the dimension named above; an argument that names none is the same for every part.
All inputs are finite; a program needn't handle non-finite values.
Results may differ from a plain program's by a relative error of at most 0.00666288.
Values are sent between devices in bfloat16 or wider.
A program may use at most 1 GiB of HBM per device.

v0:
```python
import jax
import jax.numpy as jnp
from jax import lax
from jax.sharding import PartitionSpec as P, NamedSharding


def expert_ffn(expert_in, w_gate, w_up, w_down):
    gate_act = jnp.einsum('lcd,ldf->lcf', expert_in, w_gate, preferred_element_type=jnp.float32)
    up_act = jnp.einsum('lcd,ldf->lcf', expert_in, w_up, preferred_element_type=jnp.float32)
    hidden = (jax.nn.silu(gate_act) * up_act).astype(jnp.bfloat16)
    return jnp.einsum('lcf,lfd->lcd', hidden, w_down, preferred_element_type=jnp.float32).astype(jnp.bfloat16)


def serve_rows(recv_rows, recv_gate, w_gate, w_up, w_down, expert_cap):
    member = recv_gate != 0.0
    exp_slot = jnp.cumsum(member.astype(jnp.int32), axis=0) - 1
    fan_mat = (member.T[:, None, :] & (exp_slot.T[:, None, :] == jnp.arange(expert_cap)[None, :, None])).astype(jnp.bfloat16)
    expert_in = jnp.einsum('lcr,rd->lcd', fan_mat, recv_rows, preferred_element_type=jnp.float32).astype(jnp.bfloat16)
    expert_out = expert_ffn(expert_in, w_gate, w_up, w_down)
    row_outs = jnp.einsum('lcr,lcd->lrd', fan_mat, expert_out, preferred_element_type=jnp.float32)
    dev_sum = jnp.sum(recv_gate.T[:, :, None] * row_outs, axis=0)
    return dev_sum.astype(jnp.bfloat16)


def send_tables(expert_ids, gate_vals, groups, local_count, pair_cap):
    tok_dev = expert_ids.shape[0]
    chosen = jnp.any((expert_ids // local_count)[:, :, None] == jnp.arange(groups)[None, None, :], axis=1)
    send_rank = jnp.cumsum(chosen.astype(jnp.int32), axis=0) - 1
    pack_mask = chosen.T[:, None, :] & (send_rank.T[:, None, :] == jnp.arange(pair_cap)[None, :, None])
    gate_dense = jnp.sum(jnp.where(expert_ids[:, :, None] == jnp.arange(groups * local_count)[None, None, :], gate_vals[:, :, None], 0.0), axis=1)
    gate_t = jnp.swapaxes(gate_dense.reshape(tok_dev, groups, local_count), 0, 1)
    send_gate = jnp.sum(jnp.where(pack_mask[:, :, :, None], gate_t[:, None, :, :], 0.0), axis=2)
    return pack_mask.astype(jnp.bfloat16), send_gate


def solution(mesh):
    groups = mesh.shape['ep']
    row_spec = P(('dp', 'ep'))
    expert_spec = P('ep')

    def device_step(tokens, expert_ids, gate_vals, w_gate, w_up, w_down):
        tok_dev, top_k = expert_ids.shape
        d_model = tokens.shape[1]
        local_count = w_gate.shape[0]
        pair_cap = tok_dev * (top_k // 2) // groups
        expert_cap = tok_dev * top_k // local_count
        row_count = groups * pair_cap
        pack_mat, send_gate = send_tables(expert_ids, gate_vals, groups, local_count, pair_cap)
        send_rows = jnp.einsum('qct,td->qcd', pack_mat, tokens, preferred_element_type=jnp.float32).astype(jnp.bfloat16)
        recv_rows = lax.all_to_all(send_rows, 'ep', 0, 0, tiled=True)
        recv_gate = lax.all_to_all(send_gate, 'ep', 0, 0, tiled=True)
        dev_sum = serve_rows(recv_rows.reshape(row_count, d_model), recv_gate.reshape(row_count, local_count), w_gate, w_up, w_down, expert_cap)
        returned = lax.all_to_all(dev_sum.reshape(groups, pair_cap, d_model), 'ep', 0, 0, tiled=True)
        moe_sum = jnp.einsum('qct,qcd->td', pack_mat, returned, preferred_element_type=jnp.float32)
        return (tokens.astype(jnp.float32) + moe_sum).astype(jnp.bfloat16)

    return jax.shard_map(device_step, mesh=mesh, in_specs=(row_spec, row_spec, row_spec, expert_spec, expert_spec, expert_spec), out_specs=row_spec, check_vma=False)
```

profile of v0, /device:TPU:0, one launch (start us, length us, event | category | flops | bytes accessed | tf_op | source)
XLA Modules:
  0.0 240.2 jit_solution(13867545966234313817)
XLA Ops:
  0.0 0.7 add_select_fusion
  0.7 0.6 reduce-window.14
  1.3 0.2 slice_reduce_fusion.1
  1.6 0.1 copy_bitcast_fusion
  1.6 0.8 select_reduce_fusion.1
  2.4 0.1 fusion.17
  2.6 0.5 select_reduce_fusion
  3.1 0.7 reshape.69
  3.8 7.4 %all-to-all-start = ((f32[16,1,192]{2,1,0:T(1,128)}), f32[16,1,192]{2,1,0:T(1,128)S(1)}, u32[]{:S(2)}, u32[]{:S(2)}) async-start(f32[16,1,192]{2,1,0:T(1,128)} %reshape.69), calls=%async_computation | async-start | bytes 32768 | tf_op jit(solution)/shard_map/all_to_all | solution.py:51
  11.3 3.9 %convolution_convert_fusion = bf16[16,48,2048]{2,1,0:T(8,128)(2,1)} fusion(bf16[256,2048]{1,0:T(8,128)(2,1)} %param.6, s32[16,256]{1,0:T(8,128)S(1)} %copy_bitcast_fusion, pred[16,256]{1,0:T(8,128)(4,1)S(1)} %bitcast.66), kind=kOutput, calls=%fused_computation.7 | convolution fusion | flops 807272448 | bytes 4214784 | tf_op jit(solution)/shard_map/qct,td->qcd/dot_general | solution.py:49
  15.1 2.4 %all-to-all-done = f32[16,1,192]{2,1,0:T(1,128)S(1)} async-done(((f32[16,1,192]{2,1,0:T(1,128)}), f32[16,1,192]{2,1,0:T(1,128)S(1)}, u32[]{:S(2)}, u32[]{:S(2)}) %all-to-all-start) | async-done | bytes 12320 | tf_op jit(solution)/shard_map/all_to_all | solution.py:51
  17.6 3.9 %all-to-all-start.1 = ((bf16[16,48,2048]{2,1,0:T(8,128)(2,1)}), bf16[16,48,2048]{2,1,0:T(8,128)(2,1)S(1)}, u32[]{:S(2)}, u32[]{:S(2)}) async-start(bf16[16,48,2048]{2,1,0:T(8,128)(2,1)} %convolution_convert_fusion), calls=%async_computation.1 | async-start | bytes 6291456 | tf_op jit(solution)/shard_map/all_to_all | solution.py:50
  21.5 0.5 broadcast.66
  22.0 0.7 reduce.4
  22.7 0.1 reshape.70
  22.8 0.1 reshape.58
  22.9 1.1 reduce-window.16
  24.1 0.2 slice_reduce_fusion
  24.3 0.2 reduce-window.19
  24.5 0.1 add_bitcast_fusion
  24.6 56.2 %all-to-all-done.1 = bf16[16,48,2048]{2,1,0:T(8,128)(2,1)S(1)} async-done(((bf16[16,48,2048]{2,1,0:T(8,128)(2,1)}), bf16[16,48,2048]{2,1,0:T(8,128)(2,1)S(1)}, u32[]{:S(2)}, u32[]{:S(2)}) %all-to-all-start.1) | async-done | bytes 3145760 | tf_op jit(solution)/shard_map/all_to_all | solution.py:50
  80.8 7.7 %fusion.5 = bf16[4,384,2048]{2,1,0:T(8,128)(2,1)} fusion(bf16[768,2048,1]{1,0,2:T(8,128)(2,1)S(1)} %bitcast.60, s32[4,768]{1,0:T(4,128)S(1)} %bitcast.69, pred[4,768]{1,0:T(4,128)(4,1)S(1)} %get-tuple-element.6), kind=kOutput, calls=%fused_computation.6 | convolution fusion | flops 4837343232 | bytes 9452544 | tf_op jit(solution)/shard_map/lcr,rd->lcd/dot_general | solution.py:18
  88.5 18.4 %fusion.24 = f32[4,384,1408]{2,1,0:T(8,128)} fusion(bf16[4,384,2048]{2,1,0:T(8,128)(2,1)} %fusion.5, bf16[4,2048,1408]{2,1,0:T(8,128)(2,1)} %param.9), kind=kOutput, calls=%fused_computation.41 | convolution fusion | flops 8858370048 | bytes 38010880 | tf_op jit(solution)/shard_map/lcd,ldf->lcf/dot_general | solution.py:8
  106.9 21.4 %multiply_convert_fusion = bf16[4,384,1408]{2,1,0:T(8,128)(2,1)} fusion(f32[4,384,1408]{2,1,0:T(8,128)} %fusion.24, bf16[4,384,2048]{2,1,0:T(8,128)(2,1)} %fusion.5, bf16[4,2048,1408]{2,1,0:T(8,128)(2,1)} %param.10), kind=kOutput, calls=%fused_computation.1 | convolution fusion | flops 8871346176 | bytes 42336256 | tf_op jit(solution)/shard_map/lcd,ldf->lcf/dot_general | solution.py:9
  128.3 15.7 %fusion.47 = bf16[4,384,2048]{2,1,0:T(8,128)(2,1)S(1)} fusion(bf16[4,384,1408]{2,1,0:T(8,128)(2,1)} %multiply_convert_fusion, bf16[4,1408,2048]{2,1,0:T(8,128)(2,1)} %param.11), kind=kOutput, calls=%fused_computation.2.clone.2 | convolution fusion | flops 8861515776 | bytes 33685504 | tf_op jit(solution)/shard_map/lcf,lfd->lcd/dot_general | solution.py:11
  144.0 8.2 %multiply_reduce_fusion = bf16[768,2048]{1,0:T(8,128)(2,1)S(1)} fusion(f32[4,768]{1,0:T(4,128)S(1)} %bitcast.68, s32[4,768]{1,0:T(4,128)S(1)} %bitcast.70, pred[4,768]{1,0:T(4,128)(4,1)S(1)} %get-tuple-element.6, bf16[4,384,2048]{2,1,0:T(8,128)(2,1)S(1)} %fusion.47), kind=kOutput, calls=%fused_computation | convolution fusion | flops 4845207552 | bytes 9464832 | tf_op jit(solution)/shard_map/lcr,lcd->lrd/dot_general | solution.py:20
  152.1 0.0 copy-start
  152.1 86.0 %all_to_all.15 = bf16[16,48,2048]{2,1,0:T(8,128)(2,1)S(1)} all-to-all(bf16[16,48,2048]{2,1,0:T(8,128)(2,1)S(1)} %bitcast.61), channel_id=1, replica_groups=mesh['dp'=2,'ep'=16] {'ep'}, dimensions={0} | all-to-all | bytes 6291456 | tf_op jit(solution)/shard_map/all_to_all | solution.py:53
  238.2 0.0 copy-done
  238.2 2.0 fusion.11
  (9 shorter events, 0.1 us)
Async XLA Ops:
  3.8 13.8 %all-to-all-start = ((f32[16,1,192]{2,1,0:T(1,128)}), f32[16,1,192]{2,1,0:T(1,128)S(1)}, u32[]{:S(2)}, u32[]{:S(2)}) async-start(f32[16,1,192]{2,1,0:T(1,128)} %reshape.69), calls=%async_computation | async-start | bytes 32768 | tf_op jit(solution)/shard_map/all_to_all | solution.py:51
  17.6 63.2 %all-to-all-start.1 = ((bf16[16,48,2048]{2,1,0:T(8,128)(2,1)}), bf16[16,48,2048]{2,1,0:T(8,128)(2,1)S(1)}, u32[]{:S(2)}, u32[]{:S(2)}) async-start(bf16[16,48,2048]{2,1,0:T(8,128)(2,1)} %convolution_convert_fusion), calls=%async_computation.1 | async-start | bytes 6291456 | tf_op jit(solution)/shard_map/all_to_all | solution.py:50
  152.1 86.1 %copy-start = (bf16[256,2048]{1,0:T(8,128)(2,1)S(1)}, bf16[256,2048]{1,0:T(8,128)(2,1)}, u32[]{:S(2)}) copy-start(bf16[256,2048]{1,0:T(8,128)(2,1)} %param.6) | copy-start | bytes 3145732
where the time goes:
time: 241 us; the launch traced here: 240 us
  blocking collectives  86 us (36%)
  matrix products  77.2 us (32%)
  waiting for transfers between devices  58.7 us (24%)
  starting transfers between devices  11.4 us (5%)
  other arithmetic  4.96 us (2%)
    all_to_all x1, blocking collectives, device_step(): lax.all_to_all(dev_sum.reshape(groups, pair_cap, d_model), 'ep', 0, 0, ti...  86 us
    all_to_all x1, waiting for transfers between devices, device_step(): recv_rows = lax.all_to_all(send_rows, 'ep', 0, 0, tiled=True)  56.2 us
    dot_general x1, matrix products, expert_ffn(): jnp.einsum('lcd,ldf->lcf', expert_in, w_up, preferred_element_type=jnp.fl...  21.4 us
    dot_general x1, matrix products, expert_ffn(): jnp.einsum('lcd,ldf->lcf', expert_in, w_gate, preferred_element_type=jnp....  18.4 us
    dot_general x1, matrix products, expert_ffn(): jnp.einsum('lcf,lfd->lcd', hidden, w_down, preferred_element_type=jnp.flo...  15.7 us
    dot_general x1, matrix products, serve_rows(): jnp.einsum('lcr,lcd->lrd', fan_mat, expert_out, preferred_element_type=jn...  8.15 us
    dot_general x1, matrix products, serve_rows(): jnp.einsum('lcr,rd->lcd', fan_mat, recv_rows, preferred_element_type=jnp....  7.66 us
    all_to_all x1, starting transfers between devices, device_step(): recv_gate = lax.all_to_all(send_gate, 'ep', 0, 0, tiled=True)  7.45 us
  transfers between devices with their start and end apart: 2, of which 2 were waited for; matrix products, arithmetic and copies ran while one was open for 3% of the time, Pallas kernels for 0%

commit v1 on v0

v1 whole, which is shorter than its diff:
```python
import functools

import jax
import jax.numpy as jnp
from jax import lax
from jax.experimental import pallas as pl
from jax.experimental.pallas import tpu as pltpu
from jax.sharding import PartitionSpec as P

F32 = jnp.float32
BF16 = jnp.bfloat16
COLS = 256


def moe_kernel(groups, pair_cap, parts, x_ref, ids_ref, gates_ref, wg_hbm, wu_hbm, wd_hbm, out_ref,
               send_n, send_a, send_b, recv_n, recv_a, recv_b, sum_n, sum_a, sum_b, ret_n, ret_a, ret_b,
               sgate, rgate, gcol_n, gcol_a, gcol_b, pick_t, wg_buf, wu_buf, wd_buf, hid, acc, total,
               w_sem, ds_sem, dr_sem, gs_sem, gr_sem, cs_sem, cr_sem):
    me = lax.axis_index('ep')
    dp = lax.axis_index('dp')
    half_n = groups // 2
    half = me // half_n
    mine = me % half_n
    tok, d_model = x_ref.shape
    local_count, _, ffn = wg_hbm.shape
    top_k = ids_ref.shape[1]
    part_a, part_b = parts
    rows = {'n': pair_cap, 'a': part_a, 'b': part_b}
    base = {'n': 0, 'a': 0, 'b': part_a}
    send = {'n': send_n, 'a': send_a, 'b': send_b}
    recv = {'n': recv_n, 'a': recv_a, 'b': recv_b}
    sums = {'n': sum_n, 'a': sum_a, 'b': sum_b}
    ret = {'n': ret_n, 'a': ret_a, 'b': ret_b}
    gcol = {'n': gcol_n, 'a': gcol_a, 'b': gcol_b}
    row_of = {'n': 0, 'a': 1, 'b': 2}

    def device(phase, slot):
        side = half if phase == 'n' else 1 - half
        return (dp, side * half_n + slot)

    def slot_of(k):
        return lax.rem(mine + k, half_n)

    def first(phase):
        return 1 if phase == 'n' else 0

    def w_copy(which, expert, slot):
        hbm, buf = ((wg_hbm, wg_buf), (wu_hbm, wu_buf), (wd_hbm, wd_buf))[which]
        return pltpu.make_async_copy(hbm.at[expert], buf.at[slot], w_sem.at[which, slot])

    barrier = pltpu.get_barrier_semaphore()
    for k in range(1, half_n):
        pl.semaphore_signal(barrier, inc=1, device_id=device('n', slot_of(k)), device_id_type=pl.DeviceIdType.MESH)
    for k in range(half_n):
        pl.semaphore_signal(barrier, inc=1, device_id=device('a', slot_of(k)), device_id_type=pl.DeviceIdType.MESH)

    for expert in range(2):
        for which in range(3):
            w_copy(which, expert, expert).start()

    ids_t = ids_ref[...].T
    slot_ids = (ids_t + half * (half_n * local_count)) % (groups * local_count)
    slot_dev = slot_ids // local_count
    dev_iota = lax.broadcasted_iota(jnp.int32, (groups, tok), 0)
    chosen = dev_iota == slot_dev[0:1, :]
    for j in range(1, top_k):
        chosen = chosen | (dev_iota == slot_dev[j:j + 1, :])
    tri = (lax.broadcasted_iota(jnp.int32, (tok, tok), 0) <= lax.broadcasted_iota(jnp.int32, (tok, tok), 1)).astype(F32).astype(BF16)
    rank = jnp.dot(chosen.astype(F32).astype(BF16), tri, preferred_element_type=F32)
    rank = jnp.where(chosen, rank - 1.0, -1.0)

    def pick(phase):
        lo = 0 if phase == 'n' else half_n
        c_iota = lax.broadcasted_iota(jnp.int32, (half_n, rows[phase], tok), 1).astype(F32) + float(base[phase])
        mask = rank[lo:lo + half_n].reshape(half_n, 1, tok) == c_iota
        return mask.astype(F32).reshape(half_n * rows[phase], tok)

    def pack(phase):
        m = half_n * rows[phase]
        mat = pick(phase).astype(BF16)
        for n in range(0, d_model, COLS):
            part = jnp.dot(mat, x_ref[:, n:n + COLS], preferred_element_type=F32).astype(BF16)
            send[phase][:, :, n:n + COLS] = part.reshape(half_n, rows[phase], COLS)

    def row_copy(phase, slot):
        i = row_of[phase]
        return pltpu.make_async_remote_copy(
            src_ref=send[phase].at[slot], dst_ref=recv[phase].at[mine], send_sem=ds_sem.at[i, slot], recv_sem=dr_sem.at[i, mine],
            device_id=device(phase, slot), device_id_type=pl.DeviceIdType.MESH)

    def row_arrival(phase, slot):
        i = row_of[phase]
        return pltpu.make_async_remote_copy(
            src_ref=send[phase].at[slot], dst_ref=recv[phase].at[slot], send_sem=ds_sem.at[i, slot], recv_sem=dr_sem.at[i, slot],
            device_id=device(phase, slot), device_id_type=pl.DeviceIdType.MESH)

    def gate_copy(phase, slot, arrival=False):
        lo = 0 if phase == 'n' else half_n
        at = slot if arrival else mine
        return pltpu.make_async_remote_copy(
            src_ref=sgate.at[lo + slot], dst_ref=rgate.at[lo + at], send_sem=gs_sem.at[lo + slot], recv_sem=gr_sem.at[lo + at],
            device_id=device(phase, slot), device_id_type=pl.DeviceIdType.MESH)

    def sum_copy(phase, slot, arrival=False):
        i = row_of[phase]
        at = slot if arrival else mine
        return pltpu.make_async_remote_copy(
            src_ref=sums[phase].at[slot], dst_ref=ret[phase].at[at], send_sem=cs_sem.at[i, slot], recv_sem=cr_sem.at[i, at],
            device_id=device(phase, slot), device_id_type=pl.DeviceIdType.MESH)

    pack('n')
    pl.semaphore_wait(barrier, groups - 1)
    for k in range(1, half_n):
        row_copy('n', slot_of(k)).start()
    for phase in ('a', 'b'):
        pack(phase)
        for k in range(half_n):
            row_copy(phase, slot_of(k)).start()

    gates_t = gates_ref[...].T
    gd_row = lax.broadcasted_iota(jnp.int32, (groups * 8, tok), 0)
    gd_id = jnp.where(gd_row % 8 < local_count, (gd_row // 8) * local_count + gd_row % 8, -1)
    dense = jnp.zeros((groups * 8, tok), F32)
    for j in range(top_k):
        dense = dense + jnp.where(gd_id == slot_ids[j:j + 1, :], gates_t[j:j + 1, :], 0.0)
    lane_iota = lax.broadcasted_iota(jnp.int32, (128, tok), 0).astype(F32)
    for s in range(groups):
        mat = (rank[s:s + 1, :] == lane_iota).astype(F32)
        sgate[s] = lax.dot_general(dense[s * 8:(s + 1) * 8], mat, (((1,), (1,)), ((), ())),
                                   precision=lax.Precision.HIGHEST, preferred_element_type=F32)
    for k in range(1, half_n):
        gate_copy('n', slot_of(k)).start()
    for k in range(half_n):
        gate_copy('a', slot_of(k)).start()
    rgate[mine] = sgate[mine]
    recv_n[mine] = send_n[mine]

    col = 0
    cols_of = {}
    for phase in ('n', 'a', 'b'):
        m = half_n * rows[phase]
        pick_t[:, col:col + m] = pick(phase).T.astype(BF16)
        cols_of[phase] = (col, col + m)
        col += m

    def gate_columns(phase):
        lo = 0 if phase == 'n' else half_n
        for s in range(half_n):
            tile = rgate[lo + s].T
            gcol[phase][s * rows[phase]:(s + 1) * rows[phase], 0:8] = tile[base[phase]:base[phase] + rows[phase], :]

    def ffn_pass(phase, last):
        m = half_n * rows[phase]
        x_in = recv[phase]

        def step(expert, carry):
            slot = lax.rem(expert, 2)
            nxt = lax.rem(expert + 2, local_count)

            def refill(which):
                if last:
                    @pl.when(expert < local_count - 2)
                    def _():
                        w_copy(which, nxt, slot).start()
                else:
                    w_copy(which, nxt, slot).start()

            w_copy(0, expert, slot).wait()
            w_copy(1, expert, slot).wait()
            lhs = x_in[...].reshape(m, d_model)
            for n in range(0, ffn, COLS):
                w = min(COLS, ffn - n)
                g = jnp.dot(lhs, wg_buf[slot, :, n:n + w], preferred_element_type=F32)
                u = jnp.dot(lhs, wu_buf[slot, :, n:n + w], preferred_element_type=F32)
                hid[0:m, n:n + w] = (jax.nn.silu(g) * u).astype(BF16)
            refill(0)
            refill(1)
            w_copy(2, expert, slot).wait()
            gc = gcol[phase][...]
            g_col = jnp.sum(jnp.where(lax.broadcasted_iota(jnp.int32, gc.shape, 1) == expert, gc, 0.0), axis=1, keepdims=True)
            hv = hid[0:m, :]
            for n in range(0, d_model, COLS):
                y = jnp.dot(hv, wd_buf[slot, :, n:n + COLS], preferred_element_type=F32).astype(BF16).astype(F32)
                acc[0:m, n:n + COLS] = acc[0:m, n:n + COLS] + jnp.where(g_col > 0.0, g_col * y, 0.0)
            refill(2)
            return carry

        acc[0:m, :] = jnp.zeros((m, d_model), F32)
        lax.fori_loop(0, local_count, step, 0)
        sums[phase][...] = acc[0:m, :].astype(BF16).reshape(half_n, rows[phase], d_model)

    for phase in ('n', 'a', 'b'):
        for k in range(first(phase), half_n):
            row_arrival(phase, slot_of(k)).wait_recv()
            if phase != 'b':
                gate_copy(phase, slot_of(k), arrival=True).wait_recv()
        gate_columns(phase)
        ffn_pass(phase, phase == 'b')
        for k in range(first(phase), half_n):
            sum_copy(phase, slot_of(k)).start()
    ret_n[mine] = sum_n[mine]

    for phase in ('n', 'a', 'b'):
        for k in range(first(phase), half_n):
            sum_copy(phase, slot_of(k), arrival=True).wait_recv()
        m = half_n * rows[phase]
        lo, hi = cols_of[phase]
        got = ret[phase][...].reshape(m, d_model)
        pt = pick_t[:, lo:hi]
        for n in range(0, d_model, COLS):
            part = jnp.dot(pt, got[:, n:n + COLS], preferred_element_type=F32)
            if phase == 'n':
                total[:, n:n + COLS] = x_ref[:, n:n + COLS].astype(F32) + part
            elif phase == 'a':
                total[:, n:n + COLS] = total[:, n:n + COLS] + part
            else:
                out_ref[:, n:n + COLS] = (total[:, n:n + COLS] + part).astype(BF16)

    for phase in ('n', 'a', 'b'):
        for k in range(first(phase), half_n):
            row_copy(phase, slot_of(k)).wait_send()
            if phase != 'b':
                gate_copy(phase, slot_of(k)).wait_send()
            sum_copy(phase, slot_of(k)).wait_send()


def solution(mesh):
    groups = mesh.shape['ep']
    row_spec = P(('dp', 'ep'))
    expert_spec = P('ep')

    def device_step(tokens, expert_ids, gate_vals, w_gate, w_up, w_down):
        tok, top_k = expert_ids.shape
        d_model = tokens.shape[1]
        local_count, _, ffn = w_gate.shape
        pair_cap = tok * (top_k // 2) // groups
        part_b = (pair_cap // 3) // 16 * 16
        part_a = pair_cap - part_b
        half_n = groups // 2
        sizes = (pair_cap, part_a, part_b)

        def row_bufs():
            return [pltpu.VMEM((half_n, r, d_model), BF16) for r in sizes]

        scratch = row_bufs() + row_bufs() + row_bufs() + row_bufs() + [
            pltpu.VMEM((groups, 8, 128), F32),
            pltpu.VMEM((groups, 8, 128), F32),
        ] + [pltpu.VMEM((half_n * r, 8), F32) for r in sizes] + [
            pltpu.VMEM((tok, groups * pair_cap), BF16),
            pltpu.VMEM((2, d_model, ffn), BF16),
            pltpu.VMEM((2, d_model, ffn), BF16),
            pltpu.VMEM((2, ffn, d_model), BF16),
            pltpu.VMEM((half_n * pair_cap, ffn), BF16),
            pltpu.VMEM((half_n * pair_cap, d_model), F32),
            pltpu.VMEM((tok, d_model), F32),
            pltpu.SemaphoreType.DMA((3, 2)),
            pltpu.SemaphoreType.DMA((3, half_n)),
            pltpu.SemaphoreType.DMA((3, half_n)),
            pltpu.SemaphoreType.DMA((groups,)),
            pltpu.SemaphoreType.DMA((groups,)),
            pltpu.SemaphoreType.DMA((3, half_n)),
            pltpu.SemaphoreType.DMA((3, half_n)),
        ]
        vmem = pl.BlockSpec(memory_space=pltpu.VMEM)
        hbm = pl.BlockSpec(memory_space=pl.ANY)
        return pl.pallas_call(
            functools.partial(moe_kernel, groups, pair_cap, (part_a, part_b)),
            out_shape=jax.ShapeDtypeStruct((tok, d_model), BF16),
            in_specs=[vmem, vmem, vmem, hbm, hbm, hbm],
            out_specs=vmem,
            scratch_shapes=scratch,
            compiler_params=pltpu.CompilerParams(collective_id=0, has_side_effects=True, vmem_limit_bytes=66_000_000),
            name='moe_exchange',
        )(tokens, expert_ids, gate_vals, w_gate, w_up, w_down)

    return jax.shard_map(device_step, mesh=mesh, in_specs=(row_spec, row_spec, row_spec, expert_spec, expert_spec, expert_spec), out_specs=row_spec, check_vma=False)
```

time: 241 us -> 183 us (0.76)
  Pallas kernels: 0 us -> 177 us
  blocking collectives: 86 us -> 0 us
  matrix products: 77.2 us -> 0 us
  waiting for transfers between devices: 58.7 us -> 0 us
  starting transfers between devices: 11.4 us -> 0 us
  other arithmetic: 4.96 us -> 0 us
  local copies, waits for them, and re-layouts: 1.85 us -> 5.28 us
    pallas_call x0 -> x1, Pallas kernels: none -> 177 us  [device_step(): pl.pallas_call(functools.partial(moe_kernel, groups, pair_cap, (part_a, p...]
    all_to_all x1 -> x0, blocking collectives: 86 us -> none  [device_step(): lax.all_to_all(dev_sum.reshape(groups, pair_cap, d_model), 'ep', 0, 0, ti...]
    dot_general x7 -> x0, matrix products: 77.2 us -> none  [the longest x1 21.4 us: expert_ffn(): jnp.einsum('lcd,ldf->lcf', expert_in, w_up, preferred_element_type=jnp.fl...]
    all_to_all x2 -> x0, waiting for transfers between devices: 58.7 us -> none  [the longest x1 56.2 us: device_step(): recv_rows = lax.all_to_all(send_rows, 'ep', 0, 0, tiled=True)]
    all_to_all x2 -> x0, starting transfers between devices: 11.4 us -> none  [the longest x1 7.45 us: device_step(): recv_gate = lax.all_to_all(send_gate, 'ep', 0, 0, tiled=True)]
    unnamed x5 -> x3, local copies, waits for them, and re-layouts: 0.81 us -> 5.28 us
  transfers between devices with their start and end apart: 2 -> 0, of which waited for: 2 -> 0; matrix products, arithmetic and copies ran while one was open for 3% -> 0% of each run, Pallas kernels for 0% -> 0%
where the time goes in v1:
time: 183 us; the launch traced here: 182 us
  Pallas kernels  177 us (97%)
  local copies, waits for them, and re-layouts  5.28 us (3%)
    pallas_call x1, Pallas kernels, device_step(): pl.pallas_call(functools.partial(moe_kernel, groups, pair_cap, (part_a, p...  177 us
    unnamed x3, local copies, waits for them, and re-layouts  5.28 us

profile of v1, /device:TPU:0, one launch (start us, length us, event | category | flops | bytes accessed | tf_op | source)
XLA Modules:
  0.0 182.3 jit_solution(9553107577613637774)
XLA Ops:
  0.0 1.5 copy.7.ids_ref
  1.5 1.5 copy.8.gates_ref
  3.0 177.0 %moe_exchange.1 = bf16[256,2048]{1,0:T(8,128)(2,1)} custom-call(bf16[256,2048]{1,0:T(8,128)(2,1)} %x_ref.1, s32[256,6]{1,0:T(8,128)} %copy.7.ids_ref, f32[256,6]{1,0:T(8,128)} %copy.8.gates_ref, bf16[4,2048,1408]{2,1,0:T(8,128)(2,1)} %wg_hbm.1, bf16[4,2048,1408]{2,1,0:T(8,128)(2,1)} %wu_hbm.1, bf16[4,1408,2048]{2,1,0:T(8,128)(2,1)} %wd_hbm.1), custom_call_target="tpu_custom_call" | custom-call | tf_op jit(solution)/shard_map/moe_exchange/pallas_call | solution.py:266
  180.0 2.3 %copy.10 = bf16[256,2048]{1,0:T(8,128)(2,1)} copy(bf16[256,2048]{1,0:T(8,128)(2,1)} %moe_exchange.1) | data formatting | bytes 2097152

commit v2 on v0

v2 whole, which is shorter than its diff:
```python
import functools

import jax
import jax.numpy as jnp
from jax import lax
from jax.experimental import pallas as pl
from jax.experimental.pallas import tpu as pltpu
from jax.sharding import PartitionSpec as P

F32 = jnp.float32
BF16 = jnp.bfloat16
COLS = 256
MESH_ID = pl.DeviceIdType.MESH


def moe_kernel(groups, pair_cap, x_ref, ids_ref, gates_ref, wg_hbm, wu_hbm, wd_hbm, out_ref,
               send, recv, sums, ret, sgate, rgate, gcol, pick_t, wg_buf, wu_buf, wd_buf, hid, acc, total,
               w_sem, ds_sem, dr_sem, gs_sem, gr_sem, cs_sem, cr_sem):
    me = lax.axis_index('ep')
    dp = lax.axis_index('dp')
    half_n = groups // 2
    quart = groups // 4
    half = me // half_n
    mine = me % half_n
    column = mine // quart
    tok, d_model = x_ref.shape
    local_count, _, ffn = wg_hbm.shape
    top_k = ids_ref.shape[0]
    m = quart * pair_cap
    base = {'y': quart * column, 'z': quart * (1 - column), 'a': half_n + quart * half, 'b': half_n + quart * (1 - half)}
    phases = ('y', 'b', 'z', 'a')

    def flip(k):
        slot, bit = 0, 1
        while bit < half_n:
            own = (mine // bit) % 2
            slot = slot + (1 - own if (k // bit) % 2 else own) * bit
            bit *= 2
        return slot

    near_y = [flip(k) for k in range(1, quart)]
    near_z = [flip(k) for k in range(quart, half_n)]
    far = [half_n + flip(k) for k in range(half_n)]
    members = {'y': near_y, 'z': near_z,
               'a': [base['a'] + flip(j) % quart for j in range(quart)], 'b': [base['b'] + flip(j) % quart for j in range(quart)]}

    def device(idx):
        side = idx // half_n
        return (dp, ((half + side) % 2) * half_n + idx % half_n)

    def own_at(idx):
        return (idx // half_n) * half_n + mine

    def w_copy(which, expert, slot):
        hbm, buf = ((wg_hbm, wg_buf), (wu_hbm, wu_buf), (wd_hbm, wd_buf))[which]
        return pltpu.make_async_copy(hbm.at[expert], buf.at[slot], w_sem.at[which, slot])

    def remote(src, dst, s_sem, r_sem, idx, arrival):
        at = idx if arrival else own_at(idx)
        return pltpu.make_async_remote_copy(
            src_ref=src.at[idx], dst_ref=dst.at[at], send_sem=s_sem.at[idx], recv_sem=r_sem.at[at],
            device_id=device(idx), device_id_type=MESH_ID)

    def row_copy(idx, arrival=False):
        return remote(send, recv, ds_sem, dr_sem, idx, arrival)

    def gate_copy(idx, arrival=False):
        return remote(sgate, rgate, gs_sem, gr_sem, idx, arrival)

    def sum_copy(idx, arrival=False):
        return remote(sums, ret, cs_sem, cr_sem, idx, arrival)

    barrier = pltpu.get_barrier_semaphore()
    others = near_y + near_z + far
    for idx in others:
        pl.semaphore_signal(barrier, inc=1, device_id=device(idx), device_id_type=MESH_ID)

    for expert in range(2):
        for which in range(3):
            w_copy(which, expert, expert).start()

    slot_ids = (ids_ref[...] + half * (half_n * local_count)) % (groups * local_count)
    slot_dev = slot_ids // local_count
    dev_iota = lax.broadcasted_iota(jnp.int32, (groups, tok), 0)
    chosen = dev_iota == slot_dev[0:1, :]
    for j in range(1, top_k):
        chosen = chosen | (dev_iota == slot_dev[j:j + 1, :])
    tri = (lax.broadcasted_iota(jnp.int32, (tok, tok), 0) <= lax.broadcasted_iota(jnp.int32, (tok, tok), 1)).astype(F32).astype(BF16)
    rank = jnp.dot(chosen.astype(F32).astype(BF16), tri, preferred_element_type=F32)
    rank = jnp.where(chosen, rank - 1.0, -1.0)

    def pick(lo, hi):
        c_iota = lax.broadcasted_iota(jnp.int32, (hi - lo, pair_cap, tok), 1).astype(F32)
        mask = rank[lo:hi].reshape(hi - lo, 1, tok) == c_iota
        return mask.astype(F32).reshape((hi - lo) * pair_cap, tok)

    def pack(lo, hi):
        mat = pick(lo, hi).astype(BF16)
        for n in range(0, d_model, COLS):
            part = jnp.dot(mat, x_ref[:, n:n + COLS], preferred_element_type=F32).astype(BF16)
            send[lo:hi, :, n:n + COLS] = part.reshape(hi - lo, pair_cap, COLS)

    pack(half_n, groups)
    pl.semaphore_wait(barrier, groups - 1)
    for idx in far[:quart]:
        row_copy(idx).start()
    pack(0, half_n)
    for idx in near_y:
        row_copy(idx).start()

    gd_row = lax.broadcasted_iota(jnp.int32, (groups * 8, tok), 0)
    gd_id = jnp.where(gd_row % 8 < local_count, (gd_row // 8) * local_count + gd_row % 8, -1)
    dense = jnp.zeros((groups * 8, tok), F32)
    for j in range(top_k):
        dense = dense + jnp.where(gd_id == slot_ids[j:j + 1, :], gates_ref[j:j + 1, :], 0.0)
    lane_iota = lax.broadcasted_iota(jnp.int32, (128, tok), 0).astype(F32)
    for s in range(groups):
        mat = (rank[s:s + 1, :] == lane_iota).astype(F32)
        sgate[s] = lax.dot_general(dense[s * 8:(s + 1) * 8], mat, (((1,), (1,)), ((), ())),
                                   precision=lax.Precision.HIGHEST, preferred_element_type=F32)
    for idx in far[:quart] + near_y:
        gate_copy(idx).start()
    for idx in far[quart:] + near_z:
        row_copy(idx).start()
        gate_copy(idx).start()
    rgate[mine] = sgate[mine]
    recv[mine] = send[mine]

    for s in range(0, groups, quart):
        pick_t[s // quart] = pick(s, s + quart).T.astype(BF16)

    def ffn_pass(phase, last):
        lo = base[phase]
        for j in range(quart):
            gcol[j * pair_cap:(j + 1) * pair_cap, :] = rgate[lo + j].T[0:pair_cap, :]

        def step(expert, carry):
            slot = lax.rem(expert, 2)
            nxt = lax.rem(expert + 2, local_count)

            def refill(which):
                if last:
                    @pl.when(expert < local_count - 2)
                    def _():
                        w_copy(which, nxt, slot).start()
                else:
                    w_copy(which, nxt, slot).start()

            w_copy(0, expert, slot).wait()
            w_copy(1, expert, slot).wait()
            lhs = recv[pl.ds(lo, quart)].reshape(m, d_model)
            for n in range(0, ffn, COLS):
                w = min(COLS, ffn - n)
                g = jnp.dot(lhs, wg_buf[slot, :, n:n + w], preferred_element_type=F32)
                u = jnp.dot(lhs, wu_buf[slot, :, n:n + w], preferred_element_type=F32)
                hid[:, n:n + w] = (jax.nn.silu(g) * u).astype(BF16)
            refill(0)
            refill(1)
            w_copy(2, expert, slot).wait()
            gc = gcol[...]
            g_col = jnp.sum(jnp.where(lax.broadcasted_iota(jnp.int32, gc.shape, 1) == expert, gc, 0.0), axis=1, keepdims=True)
            hv = hid[...]
            for n in range(0, d_model, COLS):
                y = jnp.dot(hv, wd_buf[slot, :, n:n + COLS], preferred_element_type=F32).astype(BF16).astype(F32)
                acc[:, n:n + COLS] = acc[:, n:n + COLS] + jnp.where(g_col > 0.0, g_col * y, 0.0)
            refill(2)
            return carry

        acc[...] = jnp.zeros((m, d_model), F32)
        lax.fori_loop(0, local_count, step, 0)
        sums[pl.ds(lo, quart)] = acc[...].astype(BF16).reshape(quart, pair_cap, d_model)

    for phase in phases:
        for idx in members[phase]:
            row_copy(idx, arrival=True).wait_recv()
            gate_copy(idx, arrival=True).wait_recv()
        ffn_pass(phase, phase == phases[-1])
        for idx in members[phase]:
            sum_copy(idx).start()
    ret[mine] = sums[mine]

    order = ('y', 'z', 'b', 'a')
    for phase in order:
        for idx in members[phase]:
            sum_copy(idx, arrival=True).wait_recv()
        lo = base[phase]
        got = ret[pl.ds(lo, quart)].reshape(m, d_model)
        pt = pick_t[lo // quart]
        for n in range(0, d_model, COLS):
            part = jnp.dot(pt, got[:, n:n + COLS], preferred_element_type=F32)
            if phase == order[0]:
                total[:, n:n + COLS] = x_ref[:, n:n + COLS].astype(F32) + part
            elif phase != order[-1]:
                total[:, n:n + COLS] = total[:, n:n + COLS] + part
            else:
                out_ref[:, n:n + COLS] = (total[:, n:n + COLS] + part).astype(BF16)

    for idx in others:
        row_copy(idx).wait_send()
        gate_copy(idx).wait_send()
        sum_copy(idx).wait_send()


def solution(mesh):
    groups = mesh.shape['ep']
    row_spec = P(('dp', 'ep'))
    expert_spec = P('ep')

    def device_step(tokens, expert_ids, gate_vals, w_gate, w_up, w_down):
        tok, top_k = expert_ids.shape
        d_model = tokens.shape[1]
        ffn = w_gate.shape[2]
        pair_cap = tok * (top_k // 2) // groups
        quart = groups // 4
        m = quart * pair_cap
        scratch = [pltpu.VMEM((groups, pair_cap, d_model), BF16) for _ in range(4)] + [
            pltpu.VMEM((groups, 8, 128), F32),
            pltpu.VMEM((groups, 8, 128), F32),
            pltpu.VMEM((m, 8), F32),
            pltpu.VMEM((4, tok, m), BF16),
            pltpu.VMEM((2, d_model, ffn), BF16),
            pltpu.VMEM((2, d_model, ffn), BF16),
            pltpu.VMEM((2, ffn, d_model), BF16),
            pltpu.VMEM((m, ffn), BF16),
            pltpu.VMEM((m, d_model), F32),
            pltpu.VMEM((tok, d_model), F32),
            pltpu.SemaphoreType.DMA((3, 2)),
        ] + [pltpu.SemaphoreType.DMA((groups,)) for _ in range(6)]
        vmem = pl.BlockSpec(memory_space=pltpu.VMEM)
        hbm = pl.BlockSpec(memory_space=pl.ANY)
        return pl.pallas_call(
            functools.partial(moe_kernel, groups, pair_cap),
            out_shape=jax.ShapeDtypeStruct((tok, d_model), BF16),
            in_specs=[vmem, vmem, vmem, hbm, hbm, hbm],
            out_specs=vmem,
            scratch_shapes=scratch,
            compiler_params=pltpu.CompilerParams(collective_id=0, has_side_effects=True, vmem_limit_bytes=66_000_000),
            name='moe_exchange',
        )(tokens, expert_ids.T, gate_vals.T, w_gate, w_up, w_down)

    return jax.shard_map(device_step, mesh=mesh, in_specs=(row_spec, row_spec, row_spec, expert_spec, expert_spec, expert_spec), out_specs=row_spec, check_vma=False)
```

time: 241 us -> 151 us (0.63)
  the two profiles are of different devices: /device:TPU:0 before, /device:TPU:15 now
where the time goes in v2:
time: 151 us
  Pallas kernels  149 us (99%)
  local copies, waits for them, and re-layouts  2.3 us (2%)
    pallas_call x1, Pallas kernels, device_step(): pl.pallas_call(functools.partial(moe_kernel, groups, pair_cap), out_shape...  149 us

profile of v2, /device:TPU:15, one launch (start us, length us, event | category | flops | bytes accessed | tf_op | source)
XLA Modules:
  0.0 151.0 jit_solution(11088275670846120203)
XLA Ops:
  0.0 148.7 %moe_exchange.1 = bf16[256,2048]{1,0:T(8,128)(2,1)} custom-call(bf16[256,2048]{1,0:T(8,128)(2,1)} %x_ref.1, s32[6,256]{1,0:T(8,128)} %bitcast.2, f32[6,256]{1,0:T(8,128)} %bitcast.3, bf16[4,2048,1408]{2,1,0:T(8,128)(2,1)} %wg_hbm.1, bf16[4,2048,1408]{2,1,0:T(8,128)(2,1)} %wu_hbm.1, bf16[4,1408,2048]{2,1,0:T(8,128)(2,1)} %wd_hbm.1), custom_call_target="tpu_custom_call" | custom-call | tf_op jit(solution)/shard_map/moe_exchange/pallas_call | solution.py:231
  148.7 2.3 %copy.8 = bf16[256,2048]{1,0:T(8,128)(2,1)} copy(bf16[256,2048]{1,0:T(8,128)(2,1)} %moe_exchange.1) | data formatting | bytes 2097152

commit v3 on v2

--- a/solution.py
+++ b/solution.py
@@ -15,7 +15,7 @@
 
 def moe_kernel(groups, pair_cap, x_ref, ids_ref, gates_ref, wg_hbm, wu_hbm, wd_hbm, out_ref,
                send, recv, sums, ret, sgate, rgate, gcol, pick_t, wg_buf, wu_buf, wd_buf, hid, acc, total,
-               w_sem, ds_sem, dr_sem, gs_sem, gr_sem, cs_sem, cr_sem):
+               rank_out, rel_rank, rel_x, rel_send, w_sem, ds_sem, dr_sem, gs_sem, gr_sem, cs_sem, cr_sem, rel_ds, rel_s, rel_r):
     me = lax.axis_index('ep')
     dp = lax.axis_index('dp')
     half_n = groups // 2
@@ -27,8 +27,9 @@
     local_count, _, ffn = wg_hbm.shape
     top_k = ids_ref.shape[0]
     m = quart * pair_cap
-    base = {'y': quart * column, 'z': quart * (1 - column), 'a': half_n + quart * half, 'b': half_n + quart * (1 - half)}
-    phases = ('y', 'b', 'z', 'a')
+    base = {'y': quart * column, 'z': quart * (1 - column), 'f': half_n + quart * column, 'g': half_n + quart * (1 - column)}
+    phases = ('y', 'f', 'z', 'g')
+    inner = (half + column) % 2
 
     def flip(k):
         slot, bit = 0, 1
@@ -41,8 +42,8 @@
     near_y = [flip(k) for k in range(1, quart)]
     near_z = [flip(k) for k in range(quart, half_n)]
     far = [half_n + flip(k) for k in range(half_n)]
-    members = {'y': near_y, 'z': near_z,
-               'a': [base['a'] + flip(j) % quart for j in range(quart)], 'b': [base['b'] + flip(j) % quart for j in range(quart)]}
+    members = {'y': near_y, 'z': near_z, 'f': far[:quart], 'g': far[quart:]}
+    relayed = half_n + mine
 
     def device(idx):
         side = idx // half_n
@@ -63,6 +64,17 @@
 
     def row_copy(idx, arrival=False):
         return remote(send, recv, ds_sem, dr_sem, idx, arrival)
+
+    def relay_copy(slot):
+        return pltpu.make_async_remote_copy(
+            src_ref=rel_send.at[slot], dst_ref=recv.at[relayed], send_sem=rel_ds.at[slot], recv_sem=dr_sem.at[relayed],
+            device_id=device(slot), device_id_type=MESH_ID)
+
+    def relay_in(which):
+        src, dst = ((x_ref, rel_x), (rank_out, rel_rank))[which]
+        return pltpu.make_async_remote_copy(
+            src_ref=src, dst_ref=dst, send_sem=rel_s.at[which], recv_sem=rel_r.at[which],
+            device_id=device(relayed), device_id_type=MESH_ID)
 
     def gate_copy(idx, arrival=False):
         return remote(sgate, rgate, gs_sem, gr_sem, idx, arrival)
@@ -89,22 +101,35 @@
     rank = jnp.dot(chosen.astype(F32).astype(BF16), tri, preferred_element_type=F32)
     rank = jnp.where(chosen, rank - 1.0, -1.0)
 
-    def pick(lo, hi):
-        c_iota = lax.broadcasted_iota(jnp.int32, (hi - lo, pair_cap, tok), 1).astype(F32)
-        mask = rank[lo:hi].reshape(hi - lo, 1, tok) == c_iota
-        return mask.astype(F32).reshape((hi - lo) * pair_cap, tok)
-
-    def pack(lo, hi):
-        mat = pick(lo, hi).astype(BF16)
+    rank_out[...] = rank[half_n:groups]
+
+    def pick(ranks):
+        n = ranks.shape[0]
+        c_iota = lax.broadcasted_iota(jnp.int32, (n, pair_cap, tok), 1).astype(F32)
+        mask = ranks.reshape(n, 1, tok) == c_iota
+        return mask.astype(F32).reshape(n * pair_cap, tok)
+
+    def pack(ranks, src, dst, lo):
+        n_part = ranks.shape[0]
+        mat = pick(ranks).astype(BF16)
         for n in range(0, d_model, COLS):
-            part = jnp.dot(mat, x_ref[:, n:n + COLS], preferred_element_type=F32).astype(BF16)
-            send[lo:hi, :, n:n + COLS] = part.reshape(hi - lo, pair_cap, COLS)
-
-    pack(half_n, groups)
+            part = jnp.dot(mat, src[:, n:n + COLS], preferred_element_type=F32).astype(BF16)
+            dst[lo:lo + n_part, :, n:n + COLS] = part.reshape(n_part, pair_cap, COLS)
+
     pl.semaphore_wait(barrier, groups - 1)
-    for idx in far[:quart]:
-        row_copy(idx).start()
-    pack(0, half_n)
+
+    @pl.when(inner == 0)
+    def _():
+        relay_in(1).start()
+        relay_in(0).start()
+
+    @pl.when(inner == 1)
+    def _():
+        pack(rank[half_n:groups], x_ref, send, half_n)
+        for idx in far[:quart]:
+            row_copy(idx).start()
+
+    pack(rank[0:half_n], x_ref, send, 0)
     for idx in near_y:
         row_copy(idx).start()
 
@@ -118,36 +143,56 @@
         mat = (rank[s:s + 1, :] == lane_iota).astype(F32)
         sgate[s] = lax.dot_general(dense[s * 8:(s + 1) * 8], mat, (((1,), (1,)), ((), ())),
                                    precision=lax.Precision.HIGHEST, preferred_element_type=F32)
-    for idx in far[:quart] + near_y:
+    for idx in others:
         gate_copy(idx).start()
-    for idx in far[quart:] + near_z:
+    for idx in near_z:
         row_copy(idx).start()
-        gate_copy(idx).start()
+
+    @pl.when(inner == 1)
+    def _():
+        for idx in far[quart:]:
+            row_copy(idx).start()
+
     rgate[mine] = sgate[mine]
     recv[mine] = send[mine]
 
     for s in range(0, groups, quart):
-        pick_t[s // quart] = pick(s, s + quart).T.astype(BF16)
-
-    def ffn_pass(phase, last):
+        pick_t[s // quart] = pick(rank[s:s + quart]).T.astype(BF16)
+
+    def relay():
+        relay_in(1).wait_recv()
+        relay_in(0).wait_recv()
+        pack(rel_rank[...], rel_x, rel_send, 0)
+        for slot in near_z + near_y:
+            relay_copy(slot).start()
+        recv[relayed] = rel_send[mine]
+
+    def ffn_pass(phase):
         lo = base[phase]
+        turn = phases.index(phase)
         for j in range(quart):
             gcol[j * pair_cap:(j + 1) * pair_cap, :] = rgate[lo + j].T[0:pair_cap, :]
 
-        def step(expert, carry):
+        def step(i, carry):
+            expert = i if turn % 2 == 0 else local_count - 1 - i
+            nxt = expert + 2 if turn % 2 == 0 else expert - 2
             slot = lax.rem(expert, 2)
-            nxt = lax.rem(expert + 2, local_count)
 
             def refill(which):
-                if last:
-                    @pl.when(expert < local_count - 2)
+                @pl.when(i < local_count - 2)
+                def _():
+                    w_copy(which, nxt, slot).start()
+
+            def arrive(which):
+                if turn == 0:
+                    w_copy(which, expert, slot).wait()
+                else:
+                    @pl.when(i >= 2)
                     def _():
-                        w_copy(which, nxt, slot).start()
-                else:
-                    w_copy(which, nxt, slot).start()
-
-            w_copy(0, expert, slot).wait()
-            w_copy(1, expert, slot).wait()
+                        w_copy(which, expert, slot).wait()
+
+            arrive(0)
+            arrive(1)
             lhs = recv[pl.ds(lo, quart)].reshape(m, d_model)
             for n in range(0, ffn, COLS):
                 w = min(COLS, ffn - n)
@@ -156,7 +201,7 @@
                 hid[:, n:n + w] = (jax.nn.silu(g) * u).astype(BF16)
             refill(0)
             refill(1)
-            w_copy(2, expert, slot).wait()
+            arrive(2)
             gc = gcol[...]
             g_col = jnp.sum(jnp.where(lax.broadcasted_iota(jnp.int32, gc.shape, 1) == expert, gc, 0.0), axis=1, keepdims=True)
             hv = hid[...]
@@ -171,15 +216,20 @@
         sums[pl.ds(lo, quart)] = acc[...].astype(BF16).reshape(quart, pair_cap, d_model)
 
     for phase in phases:
+        if phase == 'y':
+            pl.when(inner == 1)(relay)
         for idx in members[phase]:
-            row_copy(idx, arrival=True).wait_recv()
             gate_copy(idx, arrival=True).wait_recv()
-        ffn_pass(phase, phase == phases[-1])
+            if phase == 'f' and idx is members[phase][0]:
+                pl.when(inner == 0)(lambda idx=idx: row_copy(idx, arrival=True).wait_recv())
+            else:
+                row_copy(idx, arrival=True).wait_recv()
+        ffn_pass(phase)
         for idx in members[phase]:
             sum_copy(idx).start()
     ret[mine] = sums[mine]
 
-    order = ('y', 'z', 'b', 'a')
+    order = ('y', 'z', 'f', 'g')
     for phase in order:
         for idx in members[phase]:
             sum_copy(idx, arrival=True).wait_recv()
@@ -196,9 +246,22 @@
                 out_ref[:, n:n + COLS] = (total[:, n:n + COLS] + part).astype(BF16)
 
     for idx in others:
-        row_copy(idx).wait_send()
         gate_copy(idx).wait_send()
         sum_copy(idx).wait_send()
+    for idx in near_y + near_z:
+        row_copy(idx).wait_send()
+
+    @pl.when(inner == 0)
+    def _():
+        relay_in(1).wait_send()
+        relay_in(0).wait_send()
+
+    @pl.when(inner == 1)
+    def _():
+        for idx in far:
+            row_copy(idx).wait_send()
+        for slot in near_z + near_y:
+            relay_copy(slot).wait_send()
 
 
 def solution(mesh):
@@ -224,8 +287,12 @@
             pltpu.VMEM((m, ffn), BF16),
             pltpu.VMEM((m, d_model), F32),
             pltpu.VMEM((tok, d_model), F32),
+            pltpu.VMEM((groups // 2, tok), F32),
+            pltpu.VMEM((groups // 2, tok), F32),
+            pltpu.VMEM((tok, d_model), BF16),
+            pltpu.VMEM((groups // 2, pair_cap, d_model), BF16),
             pltpu.SemaphoreType.DMA((3, 2)),
-        ] + [pltpu.SemaphoreType.DMA((groups,)) for _ in range(6)]
+        ] + [pltpu.SemaphoreType.DMA((groups,)) for _ in range(6)] + [pltpu.SemaphoreType.DMA((groups // 2,)), pltpu.SemaphoreType.DMA((2,)), pltpu.SemaphoreType.DMA((2,))]
         vmem = pl.BlockSpec(memory_space=pltpu.VMEM)
         hbm = pl.BlockSpec(memory_space=pl.ANY)
         return pl.pallas_call(

time: 151 us -> 140 us (0.927)
  the two profiles are of different devices: /device:TPU:15 before, /device:TPU:10 now
where the time goes in v3:
time: 140 us
  Pallas kernels  138 us (99%)
  local copies, waits for them, and re-layouts  2.3 us (2%)
    pallas_call x1, Pallas kernels, device_step(): pl.pallas_call(functools.partial(moe_kernel, groups, pair_cap), out_shape...  138 us

profile of v3, /device:TPU:10, one launch (start us, length us, event | category | flops | bytes accessed | tf_op | source)
XLA Modules:
  0.0 140.0 jit_solution(7980044141921418536)
XLA Ops:
  0.0 137.7 %moe_exchange.1 = bf16[256,2048]{1,0:T(8,128)(2,1)} custom-call(bf16[256,2048]{1,0:T(8,128)(2,1)} %x_ref.1, s32[6,256]{1,0:T(8,128)} %bitcast.2, f32[6,256]{1,0:T(8,128)} %bitcast.3, bf16[4,2048,1408]{2,1,0:T(8,128)(2,1)} %wg_hbm.1, bf16[4,2048,1408]{2,1,0:T(8,128)(2,1)} %wu_hbm.1, bf16[4,1408,2048]{2,1,0:T(8,128)(2,1)} %wd_hbm.1), custom_call_target="tpu_custom_call" | custom-call | tf_op jit(solution)/shard_map/moe_exchange/pallas_call | solution.py:298
  137.7 2.3 %copy.8 = bf16[256,2048]{1,0:T(8,128)(2,1)} copy(bf16[256,2048]{1,0:T(8,128)(2,1)} %moe_exchange.1) | data formatting | bytes 2097152

commit v4 on v3

--- a/solution.py
+++ b/solution.py
@@ -15,7 +15,7 @@
 
 def moe_kernel(groups, pair_cap, x_ref, ids_ref, gates_ref, wg_hbm, wu_hbm, wd_hbm, out_ref,
                send, recv, sums, ret, sgate, rgate, gcol, pick_t, wg_buf, wu_buf, wd_buf, hid, acc, total,
-               rank_out, rel_rank, rel_x, rel_send, w_sem, ds_sem, dr_sem, gs_sem, gr_sem, cs_sem, cr_sem, rel_ds, rel_s, rel_r):
+               rank_out, rel_rank, rel_x, rel_send, w_sem, ds_sem, dr_sem, gs_sem, gr_sem, cs_sem, cr_sem, rel_ds, rel_s, rel_r, go_sem):
     me = lax.axis_index('ep')
     dp = lax.axis_index('dp')
     half_n = groups // 2
@@ -27,8 +27,7 @@
     local_count, _, ffn = wg_hbm.shape
     top_k = ids_ref.shape[0]
     m = quart * pair_cap
-    base = {'y': quart * column, 'z': quart * (1 - column), 'f': half_n + quart * column, 'g': half_n + quart * (1 - column)}
-    phases = ('y', 'f', 'z', 'g')
+    base = {'y': quart * column, 'z': quart * (1 - column), 'f': half_n + quart * half, 'g': half_n + quart * (1 - half)}
     inner = (half + column) % 2
 
     def flip(k):
@@ -42,8 +41,17 @@
     near_y = [flip(k) for k in range(1, quart)]
     near_z = [flip(k) for k in range(quart, half_n)]
     far = [half_n + flip(k) for k in range(half_n)]
-    members = {'y': near_y, 'z': near_z, 'f': far[:quart], 'g': far[quart:]}
-    relayed = half_n + mine
+    members = {'y': near_y, 'z': near_z, 'f': [base['f'] + flip(k) % quart for k in range(quart)],
+               'g': [base['g'] + flip(k) % quart for k in range(quart)]}
+
+    def either(a, b):
+        return inner * a + (1 - inner) * b
+
+    base.update(p=either(base['f'], base['z']), q=either(base['z'], base['f']))
+    members.update(p=[either(a, b) for a, b in zip(members['f'], members['z'])],
+                   q=[either(b, a) for a, b in zip(members['f'], members['z'])])
+    phases = ('p', 'q', 'g', 'y')
+    relayed = (members['f'][0], members['g'][0])
 
     def device(idx):
         side = idx // half_n
@@ -65,16 +73,17 @@
     def row_copy(idx, arrival=False):
         return remote(send, recv, ds_sem, dr_sem, idx, arrival)
 
-    def relay_copy(slot):
+    def relay_copy(which, slot):
+        src, at = ((rel_send, slot), (send, half_n + slot))[which]
         return pltpu.make_async_remote_copy(
-            src_ref=rel_send.at[slot], dst_ref=recv.at[relayed], send_sem=rel_ds.at[slot], recv_sem=dr_sem.at[relayed],
+            src_ref=src.at[at], dst_ref=recv.at[relayed[which]], send_sem=rel_ds.at[which, slot], recv_sem=dr_sem.at[relayed[which]],
             device_id=device(slot), device_id_type=MESH_ID)
 
-    def relay_in(which):
-        src, dst = ((x_ref, rel_x), (rank_out, rel_rank))[which]
+    def relay_in(kind, slot):
+        src, dst = ((x_ref, rel_x), (rank_out, rel_rank))[kind]
         return pltpu.make_async_remote_copy(
-            src_ref=src, dst_ref=dst, send_sem=rel_s.at[which], recv_sem=rel_r.at[which],
-            device_id=device(relayed), device_id_type=MESH_ID)
+            src_ref=src, dst_ref=dst.at[slot], send_sem=rel_s.at[kind], recv_sem=rel_r.at[kind, slot],
+            device_id=device(members['f'][0]), device_id_type=MESH_ID)
 
     def gate_copy(idx, arrival=False):
         return remote(sgate, rgate, gs_sem, gr_sem, idx, arrival)
@@ -118,19 +127,13 @@
 
     pl.semaphore_wait(barrier, groups - 1)
 
-    @pl.when(inner == 0)
-    def _():
-        relay_in(1).start()
-        relay_in(0).start()
-
     @pl.when(inner == 1)
     def _():
-        pack(rank[half_n:groups], x_ref, send, half_n)
-        for idx in far[:quart]:
-            row_copy(idx).start()
+        relay_in(1, 0).start()
+        relay_in(0, 0).start()
 
     pack(rank[0:half_n], x_ref, send, 0)
-    for idx in near_y:
+    for idx in near_z + near_y:
         row_copy(idx).start()
 
     gd_row = lax.broadcasted_iota(jnp.int32, (groups * 8, tok), 0)
@@ -143,29 +146,39 @@
         mat = (rank[s:s + 1, :] == lane_iota).astype(F32)
         sgate[s] = lax.dot_general(dense[s * 8:(s + 1) * 8], mat, (((1,), (1,)), ((), ())),
                                    precision=lax.Precision.HIGHEST, preferred_element_type=F32)
-    for idx in others:
+    for idx in far + near_z + near_y:
         gate_copy(idx).start()
-    for idx in near_z:
-        row_copy(idx).start()
-
-    @pl.when(inner == 1)
-    def _():
-        for idx in far[quart:]:
-            row_copy(idx).start()
-
     rgate[mine] = sgate[mine]
     recv[mine] = send[mine]
 
     for s in range(0, groups, quart):
         pick_t[s // quart] = pick(rank[s:s + quart]).T.astype(BF16)
 
-    def relay():
-        relay_in(1).wait_recv()
-        relay_in(0).wait_recv()
-        pack(rel_rank[...], rel_x, rel_send, 0)
-        for slot in near_z + near_y:
-            relay_copy(slot).start()
-        recv[relayed] = rel_send[mine]
+    def relay(which):
+        relay_in(1, which).wait_recv()
+        relay_in(0, which).wait_recv()
+        buf, lo = ((rel_send, 0), (send, half_n))[which]
+        pack(rel_rank[which], rel_x.at[which], buf, lo)
+        for slot in near_y + near_z:
+            relay_copy(which, slot).start()
+        recv[relayed[which]] = buf[lo + mine]
+
+    @pl.when(inner == 1)
+    def _():
+        relay_in(1, 0).wait_send()
+        relay_in(0, 0).wait_send()
+        for idx in far:
+            gate_copy(idx).wait_send()
+        pl.semaphore_signal(go_sem, inc=1, device_id=device(near_z[0]), device_id_type=MESH_ID)
+        relay(0)
+
+    @pl.when(inner == 0)
+    def _():
+        for idx in far:
+            gate_copy(idx).wait_send()
+        pl.semaphore_wait(go_sem, 1)
+        relay_in(1, 1).start()
+        relay_in(0, 1).start()
 
     def ffn_pass(phase):
         lo = base[phase]
@@ -216,11 +229,11 @@
         sums[pl.ds(lo, quart)] = acc[...].astype(BF16).reshape(quart, pair_cap, d_model)
 
     for phase in phases:
-        if phase == 'y':
-            pl.when(inner == 1)(relay)
+        if phase == 'q':
+            pl.when(inner == 1)(lambda: relay(1))
         for idx in members[phase]:
             gate_copy(idx, arrival=True).wait_recv()
-            if phase == 'f' and idx is members[phase][0]:
+            if phase in ('p', 'g') and idx is members[phase][0]:
                 pl.when(inner == 0)(lambda idx=idx: row_copy(idx, arrival=True).wait_recv())
             else:
                 row_copy(idx, arrival=True).wait_recv()
@@ -229,7 +242,7 @@
             sum_copy(idx).start()
     ret[mine] = sums[mine]
 
-    order = ('y', 'z', 'f', 'g')
+    order = ('z', 'y', 'g', 'f')
     for phase in order:
         for idx in members[phase]:
             sum_copy(idx, arrival=True).wait_recv()
@@ -246,22 +259,21 @@
                 out_ref[:, n:n + COLS] = (total[:, n:n + COLS] + part).astype(BF16)
 
     for idx in others:
-        gate_copy(idx).wait_send()
         sum_copy(idx).wait_send()
     for idx in near_y + near_z:
         row_copy(idx).wait_send()
+        gate_copy(idx).wait_send()
 
     @pl.when(inner == 0)
     def _():
-        relay_in(1).wait_send()
-        relay_in(0).wait_send()
+        relay_in(1, 1).wait_send()
+        relay_in(0, 1).wait_send()
 
     @pl.when(inner == 1)
     def _():
-        for idx in far:
-            row_copy(idx).wait_send()
         for slot in near_z + near_y:
-            relay_copy(slot).wait_send()
+            relay_copy(0, slot).wait_send()
+            relay_copy(1, slot).wait_send()
 
 
 def solution(mesh):
@@ -288,11 +300,12 @@
             pltpu.VMEM((m, d_model), F32),
             pltpu.VMEM((tok, d_model), F32),
             pltpu.VMEM((groups // 2, tok), F32),
-            pltpu.VMEM((groups // 2, tok), F32),
-            pltpu.VMEM((tok, d_model), BF16),
+            pltpu.VMEM((2, groups // 2, tok), F32),
+            pltpu.VMEM((2, tok, d_model), BF16),
             pltpu.VMEM((groups // 2, pair_cap, d_model), BF16),
             pltpu.SemaphoreType.DMA((3, 2)),
-        ] + [pltpu.SemaphoreType.DMA((groups,)) for _ in range(6)] + [pltpu.SemaphoreType.DMA((groups // 2,)), pltpu.SemaphoreType.DMA((2,)), pltpu.SemaphoreType.DMA((2,))]
+        ] + [pltpu.SemaphoreType.DMA((groups,)) for _ in range(6)] + [
+            pltpu.SemaphoreType.DMA((2, groups // 2)), pltpu.SemaphoreType.DMA((2,)), pltpu.SemaphoreType.DMA((2, 2)), pltpu.SemaphoreType.REGULAR]
         vmem = pl.BlockSpec(memory_space=pltpu.VMEM)
         hbm = pl.BlockSpec(memory_space=pl.ANY)
         return pl.pallas_call(

time: 140 us -> 137 us (0.979)
  the two profiles are of different devices: /device:TPU:10 before, /device:TPU:0 now
where the time goes in v4:
time: 137 us
  Pallas kernels  135 us (99%)
  local copies, waits for them, and re-layouts  2.3 us (2%)
    pallas_call x1, Pallas kernels, device_step(): pl.pallas_call(functools.partial(moe_kernel, groups, pair_cap), out_shape...  135 us

profile of v4, /device:TPU:0, one launch (start us, length us, event | category | flops | bytes accessed | tf_op | source)
XLA Modules:
  0.0 137.3 jit_solution(11986229845765166524)
XLA Ops:
  0.0 135.0 %moe_exchange.1 = bf16[256,2048]{1,0:T(8,128)(2,1)} custom-call(bf16[256,2048]{1,0:T(8,128)(2,1)} %x_ref.1, s32[6,256]{1,0:T(8,128)} %bitcast.2, f32[6,256]{1,0:T(8,128)} %bitcast.3, bf16[4,2048,1408]{2,1,0:T(8,128)(2,1)} %wg_hbm.1, bf16[4,2048,1408]{2,1,0:T(8,128)(2,1)} %wu_hbm.1, bf16[4,1408,2048]{2,1,0:T(8,128)(2,1)} %wd_hbm.1), custom_call_target="tpu_custom_call" | custom-call | tf_op jit(solution)/shard_map/moe_exchange/pallas_call | solution.py:311
  135.0 2.3 %copy.8 = bf16[256,2048]{1,0:T(8,128)(2,1)} copy(bf16[256,2048]{1,0:T(8,128)(2,1)} %moe_exchange.1) | data formatting | bytes 2097152

commit v5 on v4

--- a/solution.py
+++ b/solution.py
@@ -159,7 +159,7 @@
         relay_in(0, which).wait_recv()
         buf, lo = ((rel_send, 0), (send, half_n))[which]
         pack(rel_rank[which], rel_x.at[which], buf, lo)
-        for slot in near_y + near_z:
+        for slot in near_z + near_y:
             relay_copy(which, slot).start()
         recv[relayed[which]] = buf[lo + mine]
 
@@ -167,9 +167,9 @@
     def _():
         relay_in(1, 0).wait_send()
         relay_in(0, 0).wait_send()
+        pl.semaphore_signal(go_sem, inc=1, device_id=device(near_z[0]), device_id_type=MESH_ID)
         for idx in far:
             gate_copy(idx).wait_send()
-        pl.semaphore_signal(go_sem, inc=1, device_id=device(near_z[0]), device_id_type=MESH_ID)
         relay(0)
 
     @pl.when(inner == 0)

time: 137 us -> 137 us (level)
  no operation moved by 1% of the time
where the time goes in v5:
time: 137 us
  Pallas kernels  134 us (98%)
  local copies, waits for them, and re-layouts  2.3 us (2%)
    pallas_call x1, Pallas kernels, device_step(): pl.pallas_call(functools.partial(moe_kernel, groups, pair_cap), out_shape...  134 us

profile of v5, /device:TPU:0, one launch (start us, length us, event | category | flops | bytes accessed | tf_op | source)
XLA Modules:
  0.0 136.7 jit_solution(10690353232221019179)
XLA Ops:
  0.0 134.4 %moe_exchange.1 = bf16[256,2048]{1,0:T(8,128)(2,1)} custom-call(bf16[256,2048]{1,0:T(8,128)(2,1)} %x_ref.1, s32[6,256]{1,0:T(8,128)} %bitcast.2, f32[6,256]{1,0:T(8,128)} %bitcast.3, bf16[4,2048,1408]{2,1,0:T(8,128)(2,1)} %wg_hbm.1, bf16[4,2048,1408]{2,1,0:T(8,128)(2,1)} %wu_hbm.1, bf16[4,1408,2048]{2,1,0:T(8,128)(2,1)} %wd_hbm.1), custom_call_target="tpu_custom_call" | custom-call | tf_op jit(solution)/shard_map/moe_exchange/pallas_call | solution.py:311
  134.4 2.3 %copy.8 = bf16[256,2048]{1,0:T(8,128)(2,1)} copy(bf16[256,2048]{1,0:T(8,128)(2,1)} %moe_exchange.1) | data formatting | bytes 2097152
